TPU v7x, 32 devices: a whole 2x2x4 slice. The times are simulated.
32 devices in a mesh: groups: 2 (over y), depth: 4 (over z), dirfreq: 2 (over x), shot: 2 (over core).
Axes of the slice: x: 2, y: 2, z: 4, core: 2. Of those that a mesh axis runs over, the one named last changes fastest.
Arguments:
- codes: bfloat16 [4, 2, 2, 1024, 1024], P('depth', 'dirfreq', None, 'shot'), may hold values from -128 to 127, as said below
- row_scale: float32 [4, 2, 1024], P('depth', 'dirfreq'), may hold values from 0 to 1, as said below
- refl_index: int32 [8, 1024], P(('groups', 'depth')), parts along dimension 0, may hold values from 0 to 127
- refl_table: float32 [128], replicated, may hold values from -0.3 to 0.3
- fields_in: bfloat16 [8, 2, 2, 96, 1024], P(('groups', 'depth'), 'dirfreq', None, 'shot'), parts along dimension 0, may hold values from -6 to 6
Outputs:
- wavefields: bfloat16 [8, 2, 2, 96, 1024], P(('groups', 'depth'), 'dirfreq', None, 'shot'), parts along dimension 0
There are 2 independent parts, one for each index of `groups`. A program takes and returns all parts, laid end to end along the dimension named above; an argument that names none is the same for every part. Nothing has to cross between parts.
Inputs may be any that keep to these rules, and one draw needn't show every extreme that they name: `codes`: whole numbers. `row_scale`: positive.
All inputs are finite; a program needn't handle non-finite values.
Results may differ from a plain program's by a relative error of at most 0.03.
Values may be sent and summed in bfloat16 or wider, within the bound.
A program may use at most 64 MiB of HBM per device.

v0:
```python
import jax
import jax.numpy as jnp
from jax import lax
from jax.sharding import PartitionSpec as P


def shifted(block, axis, distance):
    devices = range(lax.axis_size(axis))
    route = [(i - distance, i) for i in devices if i - distance in devices]
    return lax.ppermute(block, axis, route)


def contract(left, right):
    return lax.dot_general(
        left, right, (((1,), (1,)), ((), ())), preferred_element_type=jnp.float32
    )


def extrapolate(operator_full, scales, field):
    real_part = contract(field[0], operator_full[0]) - contract(field[1], operator_full[1])
    imag_part = contract(field[0], operator_full[1]) + contract(field[1], operator_full[0])
    return (jnp.stack([real_part, imag_part]) * scales[None, None, :]).astype(jnp.bfloat16)


def shards(codes, row_scale, refl_index, refl_table, fields_in):
    levels_axis = lax.axis_size("depth")
    depth_index = lax.axis_index("depth")
    halves = lax.axis_size("dirfreq") // 2
    is_down = lax.axis_index("dirfreq") < halves
    is_up = jnp.logical_not(is_down)
    direction_sign = jnp.where(is_down, 1.0, -1.0).astype(jnp.float32)
    operator_full = lax.all_gather(codes, "shot", axis=3, tiled=True)[0, 0]
    scales = row_scale[0, 0]
    classes = refl_table.shape[0]
    onehot = (refl_index[0][:, None] == jnp.arange(classes, dtype=jnp.int32)[None, :]).astype(
        jnp.float32
    )
    reflect = jnp.dot(onehot, refl_table, precision=lax.Precision.HIGHEST)
    transmit = 1.0 + direction_sign * reflect
    local = fields_in[0, 0]
    shots_local = local.shape[1]
    batches = 4
    width = shots_local // batches
    outgoing = jnp.where(is_down, 0.0, -reflect * local.astype(jnp.float32)).astype(jnp.bfloat16)
    incoming = shifted(outgoing, "dirfreq", -halves)
    base_down = incoming.astype(jnp.float32) + local.astype(jnp.float32)
    zeros_full = jnp.zeros_like(local)
    blank = jnp.zeros((2, width, local.shape[2]), jnp.bfloat16)

    def take(array, position):
        return lax.dynamic_slice_in_dim(array, position * width, width, 1)

    def place(array, piece, position, flag):
        kept = jnp.where(flag, piece, take(array, position))
        return lax.dynamic_update_slice_in_dim(array, kept, position * width, 1)

    def spare(field):
        return jnp.zeros_like(field)

    def apply_level(field):
        return extrapolate(operator_full, scales, field)

    def down_part(counter, state):
        carry_down, carry_up, results, saved, received = state
        position = counter - depth_index
        active = jnp.logical_and(position >= 0, position < batches)
        position = jnp.clip(position, 0, batches - 1)
        working = jnp.logical_and(active, is_down)
        sending = jnp.where(is_down, reflect * carry_down.astype(jnp.float32), 0.0).astype(
            jnp.bfloat16
        )
        arrived = shifted(sending, "dirfreq", halves)
        received = place(received, arrived, position, jnp.logical_and(active, is_up))
        mixed = (transmit * carry_down.astype(jnp.float32) + take(base_down, position)).astype(
            jnp.bfloat16
        )
        produced = lax.cond(working, apply_level, spare, mixed)
        results = place(results, produced, position, working)
        carry_down = shifted(produced, "depth", 1)
        return (carry_down, carry_up, results, saved, received)

    def up_part(counter, state, offset):
        carry_down, carry_up, results, saved, received = state
        position = counter - offset - (levels_axis - 1 - depth_index)
        active = jnp.logical_and(position >= 0, position < batches)
        position = jnp.clip(position, 0, batches - 1)
        working = jnp.logical_and(active, is_up)
        mixed = (
            transmit * carry_up.astype(jnp.float32) + take(received, position).astype(jnp.float32)
        ).astype(jnp.bfloat16)
        produced = lax.cond(working, apply_level, spare, mixed)
        results = place(results, produced, position, working)
        carry_up = shifted(produced, "depth", -1)
        return (carry_down, carry_up, results, saved, received)

    state = (blank, blank, zeros_full, zeros_full, zeros_full)
    span = levels_axis + batches - 1

    def both_parts(counter, state):
        return up_part(counter, down_part(counter, state), levels_axis)

    def late_up(counter, state):
        return up_part(counter, state, levels_axis)

    state = lax.fori_loop(0, levels_axis, down_part, state)
    state = lax.fori_loop(levels_axis, span, both_parts, state)
    state = lax.fori_loop(span, span + levels_axis, late_up, state)
    return state[2][None, None]


def solution(mesh):
    placed = (
        P("depth", "dirfreq", None, "shot", None),
        P("depth", "dirfreq", None),
        P(("groups", "depth"), None),
        P(),
        P(("groups", "depth"), "dirfreq", None, "shot", None),
    )
    return jax.shard_map(
        shards,
        mesh=mesh,
        in_specs=placed,
        out_specs=P(("groups", "depth"), "dirfreq", None, "shot", None),
        check_vma=False,
    )
```

profile of v0, /device:TPU:6, one launch (start us, length us, event | category | flops | bytes accessed | tf_op | source)
XLA Modules:
  0.0 184.9 jit_solution(10110929867561079466)
XLA Ops:
  9.4 2.5 %collective-permute-start.6 = (bf16[2,48,1024]{2,1,0:T(8,128)(2,1)S(1)}, bf16[2,48,1024]{2,1,0:T(8,128)(2,1)S(1)}, u32[]{:S(2)}, u32[]{:S(2)}) collective-permute-start(bf16[2,48,1024]{2,1,0:T(8,128)(2,1)S(1)} %fusion.142), channel_id=1, source_target_pairs={{2,0},{3,1},{6,4},{7,5},{10,8},{11,9},{14,12},{15,13},{18,16},{19,... | collective-permute-start | bytes 589832 | tf_op jit(solution)/shard_map/ppermute | solution.py:10
  11.9 4.1 %collective-permute-done.6 = bf16[2,48,1024]{2,1,0:T(8,128)(2,1)S(1)} collective-permute-done((bf16[2,48,1024]{2,1,0:T(8,128)(2,1)S(1)}, bf16[2,48,1024]{2,1,0:T(8,128)(2,1)S(1)}, u32[]{:S(2)}, u32[]{:S(2)}) %collective-permute-start.6) | collective-permute-done | bytes 196640 | tf_op jit(solution)/shard_map/ppermute | solution.py:10
  17.0 7.0 %all-gather.2.cloned.1.call-done = bf16[1,1,2,1024,1024]{4,3,2,1,0:T(8,128)(2,1)} async-done(((bf16[1,1,2,512,1024]{4,3,2,1,0:T(8,128)(2,1)}), bf16[1,1,2,1024,1024]{4,3,2,1,0:T(8,128)(2,1)}) %all-gather.2.cloned.1.call-update) | async-done | bytes 4194320 | tf_op jit(solution)/shard_map/all_gather | solution.py:32
  24.1 44.3 %while.59 = (s32[]{:T(128)}, bf16[2,12,1024]{2,1,0:T(8,128)(2,1)S(1)}, bf16[2,48,1024]{2,1,0:T(8,128)(2,1)S(1)}, bf16[2,48,1024]{2,1,0:T(8,128)(2,1)S(1)}, s32[]...) while((s32[]{:T(128)}, ...), condition=%wide.region_3.4_spmd, body=%wide.region_0.3_spmd.sunk | while | flops 100982800 | bytes 26931668 | solution.py:105
  25.5 3.4 %collective-permute-start = (bf16[2,12,1024]{2,1,0:T(8,128)(2,1)S(1)}, bf16[2,12,1024]{2,1,0:T(8,128)(2,1)S(1)}, u32[]{:S(2)}, u32[]{:S(2)}) collective-permute-start(bf16[2,12,1024]{2,1,0:T(8,128)(2,1)S(1)} %get-tuple-element.1456), channel_id=1, source_target_pairs={{0,4},{4,8},{8,12},{1,5},{5,9},{9,13},{2,6},{6,10},{10,14},{3,7},{... | collective-permute-start | bytes 147464 | tf_op jit(solution)/shard_map/while/body/eval_jaxpr/ppermute | solution.py:10
  32.2 4.2 %collective-permute-start = (bf16[2,12,1024]{2,1,0:T(8,128)(2,1)S(1)}, bf16[2,12,1024]{2,1,0:T(8,128)(2,1)S(1)}, u32[]{:S(2)}, u32[]{:S(2)}) collective-permute-start(bf16[2,12,1024]{2,1,0:T(8,128)(2,1)S(1)} %get-tuple-element.1456), channel_id=1, source_target_pairs={{0,4},{4,8},{8,12},{1,5},{5,9},{9,13},{2,6},{6,10},{10,14},{3,7},{... | collective-permute-start | bytes 147464 | tf_op jit(solution)/shard_map/while/body/eval_jaxpr/ppermute | solution.py:10
  36.9 4.0 %collective-permute-done.1 = bf16[2,12,1024]{2,1,0:T(8,128)(2,1)S(1)} collective-permute-done((bf16[2,12,1024]{2,1,0:T(8,128)(2,1)S(1)}, bf16[2,12,1024]{2,1,0:T(8,128)(2,1)S(1)}, u32[]{:S(2)}, u32[]{:S(2)}) %collective-permute-start.1) | collective-permute-done | bytes 49184 | tf_op jit(solution)/shard_map/while/body/eval_jaxpr/ppermute | solution.py:10
  42.8 4.3 %collective-permute-start = (bf16[2,12,1024]{2,1,0:T(8,128)(2,1)S(1)}, bf16[2,12,1024]{2,1,0:T(8,128)(2,1)S(1)}, u32[]{:S(2)}, u32[]{:S(2)}) collective-permute-start(bf16[2,12,1024]{2,1,0:T(8,128)(2,1)S(1)} %get-tuple-element.1456), channel_id=1, source_target_pairs={{0,4},{4,8},{8,12},{1,5},{5,9},{9,13},{2,6},{6,10},{10,14},{3,7},{... | collective-permute-start | bytes 147464 | tf_op jit(solution)/shard_map/while/body/eval_jaxpr/ppermute | solution.py:10
  47.5 7.0 %collective-permute-done.1 = bf16[2,12,1024]{2,1,0:T(8,128)(2,1)S(1)} collective-permute-done((bf16[2,12,1024]{2,1,0:T(8,128)(2,1)S(1)}, bf16[2,12,1024]{2,1,0:T(8,128)(2,1)S(1)}, u32[]{:S(2)}, u32[]{:S(2)}) %collective-permute-start.1) | collective-permute-done | bytes 49184 | tf_op jit(solution)/shard_map/while/body/eval_jaxpr/ppermute | solution.py:10
  56.3 4.3 %collective-permute-start = (bf16[2,12,1024]{2,1,0:T(8,128)(2,1)S(1)}, bf16[2,12,1024]{2,1,0:T(8,128)(2,1)S(1)}, u32[]{:S(2)}, u32[]{:S(2)}) collective-permute-start(bf16[2,12,1024]{2,1,0:T(8,128)(2,1)S(1)} %get-tuple-element.1456), channel_id=1, source_target_pairs={{0,4},{4,8},{8,12},{1,5},{5,9},{9,13},{2,6},{6,10},{10,14},{3,7},{... | collective-permute-start | bytes 147464 | tf_op jit(solution)/shard_map/while/body/eval_jaxpr/ppermute | solution.py:10
  61.0 7.0 %collective-permute-done.1 = bf16[2,12,1024]{2,1,0:T(8,128)(2,1)S(1)} collective-permute-done((bf16[2,12,1024]{2,1,0:T(8,128)(2,1)S(1)}, bf16[2,12,1024]{2,1,0:T(8,128)(2,1)S(1)}, u32[]{:S(2)}, u32[]{:S(2)}) %collective-permute-start.1) | collective-permute-done | bytes 49184 | tf_op jit(solution)/shard_map/while/body/eval_jaxpr/ppermute | solution.py:10
  68.4 59.4 %while.60 = (s32[]{:T(128)}, bf16[2,12,1024]{2,1,0:T(8,128)(2,1)S(1)}, bf16[2,12,1024]{2,1,0:T(8,128)(2,1)S(1)}, bf16[2,48,1024]{2,1,0:T(8,128)(2,1)S(1)}, bf16[...) while((s32[]{:T(128)}, ...), condition=%wide.region_9.10_spmd, body=%wide.region_4.9_spmd.sunk | while | flops 201891856 | bytes 53318376 | solution.py:106
  69.9 4.3 %collective-permute-start.2 = (bf16[2,12,1024]{2,1,0:T(8,128)(2,1)S(1)}, bf16[2,12,1024]{2,1,0:T(8,128)(2,1)S(1)}, u32[]{:S(2)}, u32[]{:S(2)}) collective-permute-start(bf16[2,12,1024]{2,1,0:T(8,128)(2,1)S(1)} %get-tuple-element.1457), channel_id=1, source_target_pairs={{0,4},{4,8},{8,12},{1,5},{5,9},{9,13},{2,6},{6,10},{10,14},{3,7},{... | collective-permute-start | bytes 147464 | tf_op jit(solution)/shard_map/while/body/eval_jaxpr/ppermute | solution.py:10
  74.6 7.1 %collective-permute-done.3 = bf16[2,12,1024]{2,1,0:T(8,128)(2,1)S(1)} collective-permute-done((bf16[2,12,1024]{2,1,0:T(8,128)(2,1)S(1)}, bf16[2,12,1024]{2,1,0:T(8,128)(2,1)S(1)}, u32[]{:S(2)}, u32[]{:S(2)}) %collective-permute-start.3) | collective-permute-done | bytes 49184 | tf_op jit(solution)/shard_map/while/body/eval_jaxpr/ppermute | solution.py:10
  83.8 4.8 %collective-permute-done.4 = bf16[2,12,1024]{2,1,0:T(8,128)(2,1)S(1)} collective-permute-done((bf16[2,12,1024]{2,1,0:T(8,128)(2,1)S(1)}, bf16[2,12,1024]{2,1,0:T(8,128)(2,1)S(1)}, u32[]{:S(2)}, u32[]{:S(2)}) %collective-permute-start.4) | collective-permute-done | bytes 49184 | tf_op jit(solution)/shard_map/while/body/eval_jaxpr/ppermute | solution.py:10
  90.0 3.9 %collective-permute-start.2 = (bf16[2,12,1024]{2,1,0:T(8,128)(2,1)S(1)}, bf16[2,12,1024]{2,1,0:T(8,128)(2,1)S(1)}, u32[]{:S(2)}, u32[]{:S(2)}) collective-permute-start(bf16[2,12,1024]{2,1,0:T(8,128)(2,1)S(1)} %get-tuple-element.1457), channel_id=1, source_target_pairs={{0,4},{4,8},{8,12},{1,5},{5,9},{9,13},{2,6},{6,10},{10,14},{3,7},{... | collective-permute-start | bytes 147464 | tf_op jit(solution)/shard_map/while/body/eval_jaxpr/ppermute | solution.py:10
  94.3 6.0 %collective-permute-done.3 = bf16[2,12,1024]{2,1,0:T(8,128)(2,1)S(1)} collective-permute-done((bf16[2,12,1024]{2,1,0:T(8,128)(2,1)S(1)}, bf16[2,12,1024]{2,1,0:T(8,128)(2,1)S(1)}, u32[]{:S(2)}, u32[]{:S(2)}) %collective-permute-start.3) | collective-permute-done | bytes 49184 | tf_op jit(solution)/shard_map/while/body/eval_jaxpr/ppermute | solution.py:10
  102.5 4.4 %collective-permute-done.4 = bf16[2,12,1024]{2,1,0:T(8,128)(2,1)S(1)} collective-permute-done((bf16[2,12,1024]{2,1,0:T(8,128)(2,1)S(1)}, bf16[2,12,1024]{2,1,0:T(8,128)(2,1)S(1)}, u32[]{:S(2)}, u32[]{:S(2)}) %collective-permute-start.4) | collective-permute-done | bytes 49184 | tf_op jit(solution)/shard_map/while/body/eval_jaxpr/ppermute | solution.py:10
  108.3 6.0 %collective-permute-start.2 = (bf16[2,12,1024]{2,1,0:T(8,128)(2,1)S(1)}, bf16[2,12,1024]{2,1,0:T(8,128)(2,1)S(1)}, u32[]{:S(2)}, u32[]{:S(2)}) collective-permute-start(bf16[2,12,1024]{2,1,0:T(8,128)(2,1)S(1)} %get-tuple-element.1457), channel_id=1, source_target_pairs={{0,4},{4,8},{8,12},{1,5},{5,9},{9,13},{2,6},{6,10},{10,14},{3,7},{... | collective-permute-start | bytes 147464 | tf_op jit(solution)/shard_map/while/body/eval_jaxpr/ppermute | solution.py:10
  117.0 10.9 %collective-permute-done.4 = bf16[2,12,1024]{2,1,0:T(8,128)(2,1)S(1)} collective-permute-done((bf16[2,12,1024]{2,1,0:T(8,128)(2,1)S(1)}, bf16[2,12,1024]{2,1,0:T(8,128)(2,1)S(1)}, u32[]{:S(2)}, u32[]{:S(2)}) %collective-permute-start.4) | collective-permute-done | bytes 49184 | tf_op jit(solution)/shard_map/while/body/eval_jaxpr/ppermute | solution.py:10
  127.8 49.5 %while.61 = (s32[]{:T(128)}, bf16[2,12,1024]{2,1,0:T(8,128)(2,1)S(1)}, bf16[2,48,1024]{2,1,0:T(8,128)(2,1)S(1)}, s32[]{:T(128)}, pred[]{:T(512)}, /*index=5*/f32...) while((s32[]{:T(128)}, ...), condition=%wide.region_13.14_spmd, body=%wide.region_10.13_spmd.sunk | while | flops 100909072 | bytes 26386836 | solution.py:107
  127.9 6.0 %conditional.11 = (bf16[2,12,1024]{2,1,0:T(8,128)(2,1)S(1)}) conditional(s32[]{:T(128)} %convert_element_type.280, () %tuple.151, (bf16[2,12,1024]{2,1,0:T(8,128)(2,1)S(1)}, bf16[2,1024,1024]{2,1,0:T(8,128)(2,1)}, f32[1,1,1024]{2,1,0:T(1,128)}) %tuple.152), branch_computations={%region_11.11_spmd, %region_12.12_spmd} | conditional | flops 100761600 | bytes 25792576 | solution.py:91
  127.9 2.4 %fusion.109 = f32[12,1024]{1,0:T(8,128)S(1)} fusion(bf16[2,1024,1024]{2,1,0:T(8,128)(2,1)} %get-tuple-element.974, bf16[2,12,1024]{2,1,0:T(8,128)(2,1)S(1)} %get-tuple-element.973), kind=kOutput, calls=%fused_computation.98 | convolution fusion | flops 25165824 | bytes 2179072 | tf_op jit(solution)/shard_map/while/body/eval_jaxpr/cond/branch_1_fun/dot_general | solution.py:14
  135.7 4.4 %collective-permute-done.5 = bf16[2,12,1024]{2,1,0:T(8,128)(2,1)S(1)} collective-permute-done((bf16[2,12,1024]{2,1,0:T(8,128)(2,1)S(1)}, bf16[2,12,1024]{2,1,0:T(8,128)(2,1)S(1)}, u32[]{:S(2)}, u32[]{:S(2)}) %collective-permute-start.5) | collective-permute-done | bytes 49184 | tf_op jit(solution)/shard_map/while/body/eval_jaxpr/ppermute | solution.py:10
  140.1 6.0 %conditional.11 = (bf16[2,12,1024]{2,1,0:T(8,128)(2,1)S(1)}) conditional(s32[]{:T(128)} %convert_element_type.280, () %tuple.151, (bf16[2,12,1024]{2,1,0:T(8,128)(2,1)S(1)}, bf16[2,1024,1024]{2,1,0:T(8,128)(2,1)}, f32[1,1,1024]{2,1,0:T(1,128)}) %tuple.152), branch_computations={%region_11.11_spmd, %region_12.12_spmd} | conditional | flops 100761600 | bytes 25792576 | solution.py:91
  140.2 2.4 %fusion.109 = f32[12,1024]{1,0:T(8,128)S(1)} fusion(bf16[2,1024,1024]{2,1,0:T(8,128)(2,1)} %get-tuple-element.974, bf16[2,12,1024]{2,1,0:T(8,128)(2,1)S(1)} %get-tuple-element.973), kind=kOutput, calls=%fused_computation.98 | convolution fusion | flops 25165824 | bytes 2179072 | tf_op jit(solution)/shard_map/while/body/eval_jaxpr/cond/branch_1_fun/dot_general | solution.py:14
  147.9 4.6 %collective-permute-done.5 = bf16[2,12,1024]{2,1,0:T(8,128)(2,1)S(1)} collective-permute-done((bf16[2,12,1024]{2,1,0:T(8,128)(2,1)S(1)}, bf16[2,12,1024]{2,1,0:T(8,128)(2,1)S(1)}, u32[]{:S(2)}, u32[]{:S(2)}) %collective-permute-start.5) | collective-permute-done | bytes 49184 | tf_op jit(solution)/shard_map/while/body/eval_jaxpr/ppermute | solution.py:10
  152.6 6.0 %conditional.11 = (bf16[2,12,1024]{2,1,0:T(8,128)(2,1)S(1)}) conditional(s32[]{:T(128)} %convert_element_type.280, () %tuple.151, (bf16[2,12,1024]{2,1,0:T(8,128)(2,1)S(1)}, bf16[2,1024,1024]{2,1,0:T(8,128)(2,1)}, f32[1,1,1024]{2,1,0:T(1,128)}) %tuple.152), branch_computations={%region_11.11_spmd, %region_12.12_spmd} | conditional | flops 100761600 | bytes 25792576 | solution.py:91
  152.6 2.4 %fusion.109 = f32[12,1024]{1,0:T(8,128)S(1)} fusion(bf16[2,1024,1024]{2,1,0:T(8,128)(2,1)} %get-tuple-element.974, bf16[2,12,1024]{2,1,0:T(8,128)(2,1)S(1)} %get-tuple-element.973), kind=kOutput, calls=%fused_computation.98 | convolution fusion | flops 25165824 | bytes 2179072 | tf_op jit(solution)/shard_map/while/body/eval_jaxpr/cond/branch_1_fun/dot_general | solution.py:14
  160.4 4.7 %collective-permute-done.5 = bf16[2,12,1024]{2,1,0:T(8,128)(2,1)S(1)} collective-permute-done((bf16[2,12,1024]{2,1,0:T(8,128)(2,1)S(1)}, bf16[2,12,1024]{2,1,0:T(8,128)(2,1)S(1)}, u32[]{:S(2)}, u32[]{:S(2)}) %collective-permute-start.5) | collective-permute-done | bytes 49184 | tf_op jit(solution)/shard_map/while/body/eval_jaxpr/ppermute | solution.py:10
  165.1 6.0 %conditional.11 = (bf16[2,12,1024]{2,1,0:T(8,128)(2,1)S(1)}) conditional(s32[]{:T(128)} %convert_element_type.280, () %tuple.151, (bf16[2,12,1024]{2,1,0:T(8,128)(2,1)S(1)}, bf16[2,1024,1024]{2,1,0:T(8,128)(2,1)}, f32[1,1,1024]{2,1,0:T(1,128)}) %tuple.152), branch_computations={%region_11.11_spmd, %region_12.12_spmd} | conditional | flops 100761600 | bytes 25792576 | solution.py:91
  172.8 4.5 %collective-permute-done.5 = bf16[2,12,1024]{2,1,0:T(8,128)(2,1)S(1)} collective-permute-done((bf16[2,12,1024]{2,1,0:T(8,128)(2,1)S(1)}, bf16[2,12,1024]{2,1,0:T(8,128)(2,1)S(1)}, u32[]{:S(2)}, u32[]{:S(2)}) %collective-permute-start.5) | collective-permute-done | bytes 49184 | tf_op jit(solution)/shard_map/while/body/eval_jaxpr/ppermute | solution.py:10
  (146 shorter events, 49.6 us)
Async XLA Ops:
  6.5 0.7 copy-start
  6.5 17.5 %all-gather.2.cloned.1.call-start = ((), (), s32[]{:S(2)}) async-start(), calls=%async_computation | async-start | bytes 6291456 | tf_op jit(solution)/shard_map/all_gather | solution.py:32
  9.4 6.6 %collective-permute-start.6 = (bf16[2,48,1024]{2,1,0:T(8,128)(2,1)S(1)}, bf16[2,48,1024]{2,1,0:T(8,128)(2,1)S(1)}, u32[]{:S(2)}, u32[]{:S(2)}) collective-permute-start(bf16[2,48,1024]{2,1,0:T(8,128)(2,1)S(1)} %fusion.142), channel_id=1, source_target_pairs={{2,0},{3,1},{6,4},{7,5},{10,8},{11,9},{14,12},{15,13},{18,16},{19,... | collective-permute-start | bytes 589832 | tf_op jit(solution)/shard_map/ppermute | solution.py:10
  24.2 6.2 %collective-permute-start.1 = (bf16[2,12,1024]{2,1,0:T(8,128)(2,1)S(1)}, bf16[2,12,1024]{2,1,0:T(8,128)(2,1)S(1)}, u32[]{:S(2)}, u32[]{:S(2)}) collective-permute-start(bf16[2,12,1024]{2,1,0:T(8,128)(2,1)S(1)} %get-tuple-element.1271), channel_id=1, source_target_pairs={{0,2},{1,3},{4,6},{5,7},{8,10},{9,11},{12,14},{13,15},{16,18},{17,... | collective-permute-start | bytes 147464 | tf_op jit(solution)/shard_map/while/body/eval_jaxpr/ppermute | solution.py:10
  25.5 5.3 %collective-permute-start = (bf16[2,12,1024]{2,1,0:T(8,128)(2,1)S(1)}, bf16[2,12,1024]{2,1,0:T(8,128)(2,1)S(1)}, u32[]{:S(2)}, u32[]{:S(2)}) collective-permute-start(bf16[2,12,1024]{2,1,0:T(8,128)(2,1)S(1)} %get-tuple-element.1456), channel_id=1, source_target_pairs={{0,4},{4,8},{8,12},{1,5},{5,9},{9,13},{2,6},{6,10},{10,14},{3,7},{... | collective-permute-start | bytes 147464 | tf_op jit(solution)/shard_map/while/body/eval_jaxpr/ppermute | solution.py:10
  30.9 10.0 %collective-permute-start.1 = (bf16[2,12,1024]{2,1,0:T(8,128)(2,1)S(1)}, bf16[2,12,1024]{2,1,0:T(8,128)(2,1)S(1)}, u32[]{:S(2)}, u32[]{:S(2)}) collective-permute-start(bf16[2,12,1024]{2,1,0:T(8,128)(2,1)S(1)} %get-tuple-element.1271), channel_id=1, source_target_pairs={{0,2},{1,3},{4,6},{5,7},{8,10},{9,11},{12,14},{13,15},{16,18},{17,... | collective-permute-start | bytes 147464 | tf_op jit(solution)/shard_map/while/body/eval_jaxpr/ppermute | solution.py:10
  32.2 9.1 %collective-permute-start = (bf16[2,12,1024]{2,1,0:T(8,128)(2,1)S(1)}, bf16[2,12,1024]{2,1,0:T(8,128)(2,1)S(1)}, u32[]{:S(2)}, u32[]{:S(2)}) collective-permute-start(bf16[2,12,1024]{2,1,0:T(8,128)(2,1)S(1)} %get-tuple-element.1456), channel_id=1, source_target_pairs={{0,4},{4,8},{8,12},{1,5},{5,9},{9,13},{2,6},{6,10},{10,14},{3,7},{... | collective-permute-start | bytes 147464 | tf_op jit(solution)/shard_map/while/body/eval_jaxpr/ppermute | solution.py:10
  41.4 13.0 %collective-permute-start.1 = (bf16[2,12,1024]{2,1,0:T(8,128)(2,1)S(1)}, bf16[2,12,1024]{2,1,0:T(8,128)(2,1)S(1)}, u32[]{:S(2)}, u32[]{:S(2)}) collective-permute-start(bf16[2,12,1024]{2,1,0:T(8,128)(2,1)S(1)} %get-tuple-element.1271), channel_id=1, source_target_pairs={{0,2},{1,3},{4,6},{5,7},{8,10},{9,11},{12,14},{13,15},{16,18},{17,... | collective-permute-start | bytes 147464 | tf_op jit(solution)/shard_map/while/body/eval_jaxpr/ppermute | solution.py:10
  42.8 12.1 %collective-permute-start = (bf16[2,12,1024]{2,1,0:T(8,128)(2,1)S(1)}, bf16[2,12,1024]{2,1,0:T(8,128)(2,1)S(1)}, u32[]{:S(2)}, u32[]{:S(2)}) collective-permute-start(bf16[2,12,1024]{2,1,0:T(8,128)(2,1)S(1)} %get-tuple-element.1456), channel_id=1, source_target_pairs={{0,4},{4,8},{8,12},{1,5},{5,9},{9,13},{2,6},{6,10},{10,14},{3,7},{... | collective-permute-start | bytes 147464 | tf_op jit(solution)/shard_map/while/body/eval_jaxpr/ppermute | solution.py:10
  55.0 13.1 %collective-permute-start.1 = (bf16[2,12,1024]{2,1,0:T(8,128)(2,1)S(1)}, bf16[2,12,1024]{2,1,0:T(8,128)(2,1)S(1)}, u32[]{:S(2)}, u32[]{:S(2)}) collective-permute-start(bf16[2,12,1024]{2,1,0:T(8,128)(2,1)S(1)} %get-tuple-element.1271), channel_id=1, source_target_pairs={{0,2},{1,3},{4,6},{5,7},{8,10},{9,11},{12,14},{13,15},{16,18},{17,... | collective-permute-start | bytes 147464 | tf_op jit(solution)/shard_map/while/body/eval_jaxpr/ppermute | solution.py:10
  56.3 12.1 %collective-permute-start = (bf16[2,12,1024]{2,1,0:T(8,128)(2,1)S(1)}, bf16[2,12,1024]{2,1,0:T(8,128)(2,1)S(1)}, u32[]{:S(2)}, u32[]{:S(2)}) collective-permute-start(bf16[2,12,1024]{2,1,0:T(8,128)(2,1)S(1)} %get-tuple-element.1456), channel_id=1, source_target_pairs={{0,4},{4,8},{8,12},{1,5},{5,9},{9,13},{2,6},{6,10},{10,14},{3,7},{... | collective-permute-start | bytes 147464 | tf_op jit(solution)/shard_map/while/body/eval_jaxpr/ppermute | solution.py:10
  68.5 13.1 %collective-permute-start.3 = (bf16[2,12,1024]{2,1,0:T(8,128)(2,1)S(1)}, bf16[2,12,1024]{2,1,0:T(8,128)(2,1)S(1)}, u32[]{:S(2)}, u32[]{:S(2)}) collective-permute-start(bf16[2,12,1024]{2,1,0:T(8,128)(2,1)S(1)} %get-tuple-element.1287), channel_id=1, source_target_pairs={{0,2},{1,3},{4,6},{5,7},{8,10},{9,11},{12,14},{13,15},{16,18},{17,... | collective-permute-start | bytes 147464 | tf_op jit(solution)/shard_map/while/body/eval_jaxpr/ppermute | solution.py:10
  69.9 14.0 %collective-permute-start.2 = (bf16[2,12,1024]{2,1,0:T(8,128)(2,1)S(1)}, bf16[2,12,1024]{2,1,0:T(8,128)(2,1)S(1)}, u32[]{:S(2)}, u32[]{:S(2)}) collective-permute-start(bf16[2,12,1024]{2,1,0:T(8,128)(2,1)S(1)} %get-tuple-element.1457), channel_id=1, source_target_pairs={{0,4},{4,8},{8,12},{1,5},{5,9},{9,13},{2,6},{6,10},{10,14},{3,7},{... | collective-permute-start | bytes 147464 | tf_op jit(solution)/shard_map/while/body/eval_jaxpr/ppermute | solution.py:10
  82.1 6.5 %collective-permute-start.4 = (bf16[2,12,1024]{2,1,0:T(8,128)(2,1)S(1)}, bf16[2,12,1024]{2,1,0:T(8,128)(2,1)S(1)}, u32[]{:S(2)}, u32[]{:S(2)}) collective-permute-start(bf16[2,12,1024]{2,1,0:T(8,128)(2,1)S(1)} %get-tuple-element.1458), channel_id=1, source_target_pairs={{4,0},{8,4},{12,8},{5,1},{9,5},{13,9},{6,2},{10,6},{14,10},{7,3},{... | collective-permute-start | bytes 147464 | tf_op jit(solution)/shard_map/while/body/eval_jaxpr/ppermute | solution.py:10
  88.6 11.7 %collective-permute-start.3 = (bf16[2,12,1024]{2,1,0:T(8,128)(2,1)S(1)}, bf16[2,12,1024]{2,1,0:T(8,128)(2,1)S(1)}, u32[]{:S(2)}, u32[]{:S(2)}) collective-permute-start(bf16[2,12,1024]{2,1,0:T(8,128)(2,1)S(1)} %get-tuple-element.1287), channel_id=1, source_target_pairs={{0,2},{1,3},{4,6},{5,7},{8,10},{9,11},{12,14},{13,15},{16,18},{17,... | collective-permute-start | bytes 147464 | tf_op jit(solution)/shard_map/while/body/eval_jaxpr/ppermute | solution.py:10
  90.0 12.5 %collective-permute-start.2 = (bf16[2,12,1024]{2,1,0:T(8,128)(2,1)S(1)}, bf16[2,12,1024]{2,1,0:T(8,128)(2,1)S(1)}, u32[]{:S(2)}, u32[]{:S(2)}) collective-permute-start(bf16[2,12,1024]{2,1,0:T(8,128)(2,1)S(1)} %get-tuple-element.1457), channel_id=1, source_target_pairs={{0,4},{4,8},{8,12},{1,5},{5,9},{9,13},{2,6},{6,10},{10,14},{3,7},{... | collective-permute-start | bytes 147464 | tf_op jit(solution)/shard_map/while/body/eval_jaxpr/ppermute | solution.py:10
  100.8 6.2 %collective-permute-start.4 = (bf16[2,12,1024]{2,1,0:T(8,128)(2,1)S(1)}, bf16[2,12,1024]{2,1,0:T(8,128)(2,1)S(1)}, u32[]{:S(2)}, u32[]{:S(2)}) collective-permute-start(bf16[2,12,1024]{2,1,0:T(8,128)(2,1)S(1)} %get-tuple-element.1458), channel_id=1, source_target_pairs={{4,0},{8,4},{12,8},{5,1},{9,5},{13,9},{6,2},{10,6},{14,10},{7,3},{... | collective-permute-start | bytes 147464 | tf_op jit(solution)/shard_map/while/body/eval_jaxpr/ppermute | solution.py:10
  107.0 7.8 %collective-permute-start.3 = (bf16[2,12,1024]{2,1,0:T(8,128)(2,1)S(1)}, bf16[2,12,1024]{2,1,0:T(8,128)(2,1)S(1)}, u32[]{:S(2)}, u32[]{:S(2)}) collective-permute-start(bf16[2,12,1024]{2,1,0:T(8,128)(2,1)S(1)} %get-tuple-element.1287), channel_id=1, source_target_pairs={{0,2},{1,3},{4,6},{5,7},{8,10},{9,11},{12,14},{13,15},{16,18},{17,... | collective-permute-start | bytes 147464 | tf_op jit(solution)/shard_map/while/body/eval_jaxpr/ppermute | solution.py:10
  108.3 8.6 %collective-permute-start.2 = (bf16[2,12,1024]{2,1,0:T(8,128)(2,1)S(1)}, bf16[2,12,1024]{2,1,0:T(8,128)(2,1)S(1)}, u32[]{:S(2)}, u32[]{:S(2)}) collective-permute-start(bf16[2,12,1024]{2,1,0:T(8,128)(2,1)S(1)} %get-tuple-element.1457), channel_id=1, source_target_pairs={{0,4},{4,8},{8,12},{1,5},{5,9},{9,13},{2,6},{6,10},{10,14},{3,7},{... | collective-permute-start | bytes 147464 | tf_op jit(solution)/shard_map/while/body/eval_jaxpr/ppermute | solution.py:10
  115.2 12.6 %collective-permute-start.4 = (bf16[2,12,1024]{2,1,0:T(8,128)(2,1)S(1)}, bf16[2,12,1024]{2,1,0:T(8,128)(2,1)S(1)}, u32[]{:S(2)}, u32[]{:S(2)}) collective-permute-start(bf16[2,12,1024]{2,1,0:T(8,128)(2,1)S(1)} %get-tuple-element.1458), channel_id=1, source_target_pairs={{4,0},{8,4},{12,8},{5,1},{9,5},{13,9},{6,2},{10,6},{14,10},{7,3},{... | collective-permute-start | bytes 147464 | tf_op jit(solution)/shard_map/while/body/eval_jaxpr/ppermute | solution.py:10
  127.9 4.7 %copy-start.4 = (bf16[2,1024,1024]{2,1,0:T(8,128)(2,1)S(1)}, bf16[2,1024,1024]{2,1,0:T(8,128)(2,1)}, u32[]{:S(2)}) copy-start(bf16[2,1024,1024]{2,1,0:T(8,128)(2,1)} %get-tuple-element.974) | copy-start | bytes 12582916 | tf_op jit(solution)/shard_map/while/body/eval_jaxpr/cond
  127.9 6.0 %copy-start.9 = (f32[1,1,1024]{2,1,0:T(1,128)S(1)}, f32[1,1,1024]{2,1,0:T(1,128)}, u32[]{:S(2)}) copy-start(f32[1,1,1024]{2,1,0:T(1,128)} %get-tuple-element.975) | copy-start | bytes 12292 | tf_op jit(solution)/shard_map/while/body/eval_jaxpr/cond
  133.9 6.2 %collective-permute-start.5 = (bf16[2,12,1024]{2,1,0:T(8,128)(2,1)S(1)}, bf16[2,12,1024]{2,1,0:T(8,128)(2,1)S(1)}, u32[]{:S(2)}, u32[]{:S(2)}) collective-permute-start(bf16[2,12,1024]{2,1,0:T(8,128)(2,1)S(1)} %get-tuple-element.1459), channel_id=1, source_target_pairs={{4,0},{8,4},{12,8},{5,1},{9,5},{13,9},{6,2},{10,6},{14,10},{7,3},{... | collective-permute-start | bytes 147464 | tf_op jit(solution)/shard_map/while/body/eval_jaxpr/ppermute | solution.py:10
  140.1 4.7 %copy-start.4 = (bf16[2,1024,1024]{2,1,0:T(8,128)(2,1)S(1)}, bf16[2,1024,1024]{2,1,0:T(8,128)(2,1)}, u32[]{:S(2)}) copy-start(bf16[2,1024,1024]{2,1,0:T(8,128)(2,1)} %get-tuple-element.974) | copy-start | bytes 12582916 | tf_op jit(solution)/shard_map/while/body/eval_jaxpr/cond
  140.1 6.0 %copy-start.9 = (f32[1,1,1024]{2,1,0:T(1,128)S(1)}, f32[1,1,1024]{2,1,0:T(1,128)}, u32[]{:S(2)}) copy-start(f32[1,1,1024]{2,1,0:T(1,128)} %get-tuple-element.975) | copy-start | bytes 12292 | tf_op jit(solution)/shard_map/while/body/eval_jaxpr/cond
  146.2 6.4 %collective-permute-start.5 = (bf16[2,12,1024]{2,1,0:T(8,128)(2,1)S(1)}, bf16[2,12,1024]{2,1,0:T(8,128)(2,1)S(1)}, u32[]{:S(2)}, u32[]{:S(2)}) collective-permute-start(bf16[2,12,1024]{2,1,0:T(8,128)(2,1)S(1)} %get-tuple-element.1459), channel_id=1, source_target_pairs={{4,0},{8,4},{12,8},{5,1},{9,5},{13,9},{6,2},{10,6},{14,10},{7,3},{... | collective-permute-start | bytes 147464 | tf_op jit(solution)/shard_map/while/body/eval_jaxpr/ppermute | solution.py:10
  152.6 4.7 %copy-start.4 = (bf16[2,1024,1024]{2,1,0:T(8,128)(2,1)S(1)}, bf16[2,1024,1024]{2,1,0:T(8,128)(2,1)}, u32[]{:S(2)}) copy-start(bf16[2,1024,1024]{2,1,0:T(8,128)(2,1)} %get-tuple-element.974) | copy-start | bytes 12582916 | tf_op jit(solution)/shard_map/while/body/eval_jaxpr/cond
  152.6 6.0 %copy-start.9 = (f32[1,1,1024]{2,1,0:T(1,128)S(1)}, f32[1,1,1024]{2,1,0:T(1,128)}, u32[]{:S(2)}) copy-start(f32[1,1,1024]{2,1,0:T(1,128)} %get-tuple-element.975) | copy-start | bytes 12292 | tf_op jit(solution)/shard_map/while/body/eval_jaxpr/cond
  158.7 6.4 %collective-permute-start.5 = (bf16[2,12,1024]{2,1,0:T(8,128)(2,1)S(1)}, bf16[2,12,1024]{2,1,0:T(8,128)(2,1)S(1)}, u32[]{:S(2)}, u32[]{:S(2)}) collective-permute-start(bf16[2,12,1024]{2,1,0:T(8,128)(2,1)S(1)} %get-tuple-element.1459), channel_id=1, source_target_pairs={{4,0},{8,4},{12,8},{5,1},{9,5},{13,9},{6,2},{10,6},{14,10},{7,3},{... | collective-permute-start | bytes 147464 | tf_op jit(solution)/shard_map/while/body/eval_jaxpr/ppermute | solution.py:10
  165.2 4.7 %copy-start.4 = (bf16[2,1024,1024]{2,1,0:T(8,128)(2,1)S(1)}, bf16[2,1024,1024]{2,1,0:T(8,128)(2,1)}, u32[]{:S(2)}) copy-start(bf16[2,1024,1024]{2,1,0:T(8,128)(2,1)} %get-tuple-element.974) | copy-start | bytes 12582916 | tf_op jit(solution)/shard_map/while/body/eval_jaxpr/cond
  165.2 6.0 %copy-start.9 = (f32[1,1,1024]{2,1,0:T(1,128)S(1)}, f32[1,1,1024]{2,1,0:T(1,128)}, u32[]{:S(2)}) copy-start(f32[1,1,1024]{2,1,0:T(1,128)} %get-tuple-element.975) | copy-start | bytes 12292 | tf_op jit(solution)/shard_map/while/body/eval_jaxpr/cond
  171.2 6.2 %collective-permute-start.5 = (bf16[2,12,1024]{2,1,0:T(8,128)(2,1)S(1)}, bf16[2,12,1024]{2,1,0:T(8,128)(2,1)S(1)}, u32[]{:S(2)}, u32[]{:S(2)}) collective-permute-start(bf16[2,12,1024]{2,1,0:T(8,128)(2,1)S(1)} %get-tuple-element.1459), channel_id=1, source_target_pairs={{4,0},{8,4},{12,8},{5,1},{9,5},{13,9},{6,2},{10,6},{14,10},{7,3},{... | collective-permute-start | bytes 147464 | tf_op jit(solution)/shard_map/while/body/eval_jaxpr/ppermute | solution.py:10
  (1 other events, 0.7 us)
Sparse Core Ops, SparseCore 0:
  8.9 15.1 all-gather.1
where the time goes:
time: 186 us; the launch traced here: 185 us
  waiting for transfers between devices  82.2 us (44%)
  starting transfers between devices  51.1 us (27%)
  matrix products  25 us (13%)
  between operations  13.5 us (7%)
  local copies, waits for them, and re-layouts  8.3 us (4%)
  other arithmetic  3.39 us (2%)
    ppermute x22, waiting for transfers between devices, shifted(): return lax.ppermute(block, axis, route)  74.5 us
    ppermute x22, starting transfers between devices, shifted(): return lax.ppermute(block, axis, route)  51.1 us
    dot_general x16, matrix products, contract(): lax.dot_general(left, right, (((1,), (1,)), ((), ())), preferred_element_...  23.8 us
    dynamic_update_slice x21, local copies, waits for them, and re-layouts, place(): return lax.dynamic_update_slice_in_dim(array, kept, position * width, 1)  7.44 us
    all_gather x1, waiting for transfers between devices, shards(): operator_full = lax.all_gather(codes, 'shot', axis=3, tiled=True)[0, 0]  7 us
  transfers between devices with their start and end apart: 23, of which 15 were waited for; matrix products, arithmetic and copies ran while one was open for 6% of the time, Pallas kernels for 0%

commit v1 on v0

v1 whole, which is shorter than its diff:
```python
import functools

import jax
import jax.numpy as jnp
from jax import lax
from jax.experimental import pallas as pl
from jax.experimental.pallas import tpu as pltpu
from jax.sharding import PartitionSpec as P

MESH = pl.DeviceIdType.MESH
BLOCK = 256


def kernel(levels, halves, chunks, rows, codes_hbm, scale_hbm, index_hbm, table_hbm, fields_hbm, out_ref,
           own, weights, fields, source, reflect, scale, index, table, chain, side, partner, result,
           load_sem, code_sem, code_send, code_recv, chain_send, chain_recv, side_send, side_recv, part_send):
    depth = lax.axis_index("depth")
    slot = lax.axis_index("dirfreq")
    core = lax.axis_index("shot")
    is_down = slot < halves
    is_up = jnp.logical_not(is_down)
    first, last = depth == 0, depth == levels - 1
    across = jnp.where(is_down, slot + halves, slot - halves)
    ahead = jnp.where(is_down, depth + 1, depth - 1)
    behind = jnp.where(is_down, depth - 1, depth + 1)
    has_next = jnp.where(is_down, jnp.logical_not(last), jnp.logical_not(first))
    has_prev = jnp.where(is_down, jnp.logical_not(first), jnp.logical_not(last))
    has_side = jnp.logical_or(is_down, jnp.logical_not(first))
    down_next = jnp.logical_and(is_down, jnp.logical_not(last))
    up_prev = jnp.logical_and(is_up, jnp.logical_not(first))
    blocks = own.shape[1] // BLOCK
    half = 2 * rows

    small = [pltpu.make_async_copy(a, b, load_sem.at[i]) for i, (a, b) in enumerate(
        ((index_hbm, index), (table_hbm, table), (scale_hbm, scale), (fields_hbm, fields)))]
    for copy in small:
        copy.start()

    def code_load(q, p):
        span = pl.ds(q * BLOCK, BLOCK)
        return pltpu.make_async_copy(codes_hbm.at[0, 0, p, span], own.at[p, span], code_sem.at[q, p])

    pieces = [(q, p) for q in range(blocks) for p in range(2)]
    for q, p in pieces:
        code_load(q, p).start()

    barrier = pltpu.get_barrier_semaphore()

    def greet(device):
        pl.semaphore_signal(barrier, inc=1, device_id=device, device_id_type=MESH)

    greet({"shot": 1 - core})
    greet({"dirfreq": across})

    @pl.when(has_next)
    def _():
        greet({"depth": ahead})

    @pl.when(has_prev)
    def _():
        greet({"depth": behind})

    @pl.when(down_next)
    def _():
        greet({"depth": depth + 1, "dirfreq": across})

    @pl.when(up_prev)
    def _():
        greet({"depth": depth - 1, "dirfreq": across})

    for copy in small[:2]:
        copy.wait()
    classes = table.shape[0]
    row = lax.broadcasted_iota(jnp.int32, (classes, classes), 0)
    column = lax.broadcasted_iota(jnp.int32, (classes, classes), 1)
    entries = jnp.broadcast_to(table[...].reshape(1, classes), (classes, classes))
    upright = jnp.sum(jnp.where(row == column, entries, 0.0), axis=1, keepdims=True)
    width = index.shape[1]
    picked = lax.broadcasted_iota(jnp.int32, (classes, width), 0) == index[...]
    reflect[...] = jnp.sum(jnp.where(picked, upright, 0.0), axis=0, keepdims=True)

    for copy in small[2:]:
        copy.wait()
    per = 16 // rows
    for m in range(chunks // per):
        for p in range(2):
            values = fields[0, 0, p, m * 16:(m + 1) * 16].astype(jnp.float32)
            for t in range(per):
                source[m * per + t, p * rows:(p + 1) * rows] = values[t * rows:(t + 1) * rows]

    wanted = (2 + has_next.astype(jnp.int32) + has_prev.astype(jnp.int32)
              + jnp.logical_or(down_next, up_prev).astype(jnp.int32))
    pl.semaphore_wait(barrier, wanted)

    def part_copy(k):
        return pltpu.make_async_remote_copy(
            src_ref=partner.at[k], dst_ref=side.at[k], send_sem=part_send.at[k], recv_sem=side_recv.at[k],
            device_id={"dirfreq": across}, device_id_type=MESH)

    @pl.when(is_up)
    def _():
        for k in range(chunks):
            partner[k] = (-reflect[...] * source[k]).astype(jnp.bfloat16)
            part_copy(k).start()

    @pl.when(jnp.logical_not(has_prev))
    def _():
        chain[...] = jnp.zeros_like(chain)

    @pl.when(jnp.logical_not(has_side))
    def _():
        side[...] = jnp.zeros_like(side)

    def code_copy(q, p):
        here = weights.at[core, q, p]
        return pltpu.make_async_remote_copy(
            src_ref=here, dst_ref=here, send_sem=code_send.at[q, p], recv_sem=code_recv.at[q, p],
            device_id={"shot": 1 - core}, device_id_type=MESH)

    def code_arrival(q, p):
        there = weights.at[1 - core, q, p]
        return pltpu.make_async_remote_copy(
            src_ref=there, dst_ref=there, send_sem=code_send.at[q, p], recv_sem=code_recv.at[q, p],
            device_id={"shot": 1 - core}, device_id_type=MESH)

    for q, p in pieces:
        code_load(q, p).wait()
        weights[core, q, p] = own[p, q * BLOCK:(q + 1) * BLOCK].T
        code_copy(q, p).start()

    def chain_copy(k):
        return pltpu.make_async_remote_copy(
            src_ref=result.at[k], dst_ref=chain.at[k], send_sem=chain_send.at[k], recv_sem=chain_recv.at[k],
            device_id={"depth": ahead}, device_id_type=MESH)

    def side_copy(k):
        return pltpu.make_async_remote_copy(
            src_ref=result.at[k], dst_ref=side.at[k], send_sem=side_send.at[k], recv_sem=side_recv.at[k],
            device_id={"depth": depth + 1, "dirfreq": across}, device_id_type=MESH)

    sign = jnp.where(is_down, 1.0, -1.0).astype(jnp.float32)

    def step(k, opening):
        @pl.when(has_side)
        def _():
            part_copy(k).wait_recv()

        @pl.when(has_prev)
        def _():
            chain_copy(k).wait_recv()

        beside = side[k].astype(jnp.float32)
        base = jnp.where(is_down, beside + source[k],
                         (reflect[...] * beside).astype(jnp.bfloat16).astype(jnp.float32))
        mixed = ((1.0 + sign * reflect[...]) * chain[k].astype(jnp.float32) + base).astype(jnp.bfloat16)
        for t in range(2):
            holder = core if t == 0 else 1 - core
            for q in range(blocks):
                if opening and t == 1:
                    code_arrival(q, 0).wait_recv()
                    code_arrival(q, 1).wait_recv()
                by_real = jnp.dot(mixed, weights[holder, q, 0], preferred_element_type=jnp.float32)
                by_imag = jnp.dot(mixed, weights[holder, q, 1], preferred_element_type=jnp.float32)
                real = by_real[:rows] - by_imag[rows:]
                imag = by_imag[:rows] + by_real[rows:]
                columns = pl.ds(pl.multiple_of((holder * blocks + q) * BLOCK, BLOCK), BLOCK)
                both = jnp.concatenate([real, imag], axis=0) * scale[0, :, columns]
                result[k, :, columns] = both.astype(jnp.bfloat16)

        @pl.when(has_next)
        def _():
            chain_copy(k).start()

        @pl.when(down_next)
        def _():
            side_copy(k).start()

    step(0, True)

    @pl.loop(1, chunks)
    def _(k):
        step(k, False)

    for m in range(chunks // per):
        for p in range(2):
            parts = [result[m * per + t].astype(jnp.float32)[p * rows:(p + 1) * rows] for t in range(per)]
            out_ref[0, 0, p, m * 16:(m + 1) * 16] = jnp.concatenate(parts, axis=0).astype(jnp.bfloat16)

    for q, p in pieces:
        code_copy(q, p).wait_send()

    @pl.when(is_up)
    def _():
        for k in range(chunks):
            part_copy(k).wait_send()

    @pl.when(has_next)
    def _():
        for k in range(chunks):
            chain_copy(k).wait_send()

    @pl.when(down_next)
    def _():
        for k in range(chunks):
            side_copy(k).wait_send()


def shards(codes, row_scale, refl_index, refl_table, fields_in):
    levels = lax.axis_size("depth")
    halves = lax.axis_size("dirfreq") // 2
    shots, width = fields_in.shape[3:]
    rows = 8
    chunks = shots // rows
    held = codes.shape[3]
    blocks = held // BLOCK
    dma = pltpu.SemaphoreType.DMA
    wave = (chunks, 2 * rows, width)
    any_space = pl.BlockSpec(memory_space=pltpu.HBM)
    return pl.pallas_call(
        functools.partial(kernel, levels, halves, chunks, rows),
        out_shape=jax.ShapeDtypeStruct(fields_in.shape, jnp.bfloat16),
        in_specs=[any_space] * 5,
        out_specs=pl.BlockSpec(memory_space=pltpu.VMEM),
        scratch_shapes=[
            pltpu.VMEM((2, held, width), jnp.bfloat16),
            pltpu.VMEM((2, blocks, 2, width, BLOCK), jnp.bfloat16),
            pltpu.VMEM(fields_in.shape, jnp.bfloat16),
            pltpu.VMEM(wave, jnp.float32),
            pltpu.VMEM((1, width), jnp.float32),
            pltpu.VMEM(row_scale.shape, jnp.float32),
            pltpu.VMEM(refl_index.shape, jnp.int32),
            pltpu.VMEM(refl_table.shape, jnp.float32),
            pltpu.VMEM(wave, jnp.bfloat16),
            pltpu.VMEM(wave, jnp.bfloat16),
            pltpu.VMEM(wave, jnp.bfloat16),
            pltpu.VMEM(wave, jnp.bfloat16),
            dma((4,)),
            dma((blocks, 2)),
            dma((blocks, 2)),
            dma((blocks, 2)),
            dma((chunks,)),
            dma((chunks,)),
            dma((chunks,)),
            dma((chunks,)),
            dma((chunks,)),
        ],
        compiler_params=pltpu.CompilerParams(collective_id=0, has_side_effects=True, vmem_limit_bytes=40 * 2**20),
    )(codes, row_scale, refl_index, refl_table, fields_in)


def solution(mesh):
    placed = (
        P("depth", "dirfreq", None, "shot", None),
        P("depth", "dirfreq", None),
        P(("groups", "depth"), None),
        P(),
        P(("groups", "depth"), "dirfreq", None, "shot", None),
    )
    return jax.shard_map(
        shards,
        mesh=mesh,
        in_specs=placed,
        out_specs=P(("groups", "depth"), "dirfreq", None, "shot", None),
        check_vma=False,
    )
```

time: 186 us -> 42.2 us (0.23)
  waiting for transfers between devices: 82.2 us -> 0 us
  starting transfers between devices: 51.1 us -> 0 us
  Pallas kernels: 0 us -> 36.7 us
  matrix products: 25 us -> 0 us
  between operations: 13.5 us -> 0.01 us
  other arithmetic: 3.39 us -> 0 us
  local copies, waits for them, and re-layouts: 8.3 us -> 5.22 us
    ppermute x22 -> x0, waiting for transfers between devices: 74.5 us -> none  [shifted(): return lax.ppermute(block, axis, route)]
    ppermute x22 -> x0, starting transfers between devices: 51.1 us -> none  [shifted(): return lax.ppermute(block, axis, route)]
    pallas_call x0 -> x1, Pallas kernels: none -> 36.7 us  [shards(): pl.pallas_call(functools.partial(kernel, levels, halves, chunks, rows), o...]
    dot_general x17 -> x0, matrix products: 25 us -> none  [the longest x16 23.8 us: contract(): lax.dot_general(left, right, (((1,), (1,)), ((), ())), preferred_element_...]
    dynamic_update_slice x21 -> x0, local copies, waits for them, and re-layouts: 7.44 us -> none  [place(): return lax.dynamic_update_slice_in_dim(array, kept, position * width, 1)]
    all_gather x1 -> x0, waiting for transfers between devices: 7 us -> none  [shards(): operator_full = lax.all_gather(codes, 'shot', axis=3, tiled=True)[0, 0]]
    unnamed x4 -> x11, local copies, waits for them, and re-layouts: 0.68 us -> 5.22 us
  transfers between devices with their start and end apart: 23 -> 0, of which waited for: 15 -> 0; matrix products, arithmetic and copies ran while one was open for 6% -> 0% of each run, Pallas kernels for 0% -> 0%
where the time goes in v1:
time: 42.2 us; the launch traced here: 41.9 us
  Pallas kernels  36.7 us (87%)
  local copies, waits for them, and re-layouts  5.22 us (12%)
    pallas_call x1, Pallas kernels, shards(): pl.pallas_call(functools.partial(kernel, levels, halves, chunks, rows), o...  36.7 us
    unnamed x11, local copies, waits for them, and re-layouts  5.22 us

profile of v1, /device:TPU:6, one launch (start us, length us, event | category | flops | bytes accessed | tf_op | source)
XLA Modules:
  0.0 41.9 jit_solution(13538944498434362052)
XLA Ops:
  0.0 0.0 copy-start
  0.0 1.6 %copy-done = bf16[1,1,2,512,1024]{4,3,2,1,0:T(8,128)(2,1)S(1)} copy-done((bf16[1,1,2,512,1024]{4,3,2,1,0:T(8,128)(2,1)S(1)}, bf16[1,1,2,512,1024]{4,3,2,1,0:T(8,128)(2,1)}, u32[]{:S(2)}) %copy-start) | copy-done | bytes 2097176
  1.6 0.0 copy-start.1
  1.6 0.9 %copy-done.1 = bf16[1,1,2,48,1024]{4,3,2,1,0:T(8,128)(2,1)S(1)} copy-done((bf16[1,1,2,48,1024]{4,3,2,1,0:T(8,128)(2,1)S(1)}, bf16[1,1,2,48,1024]{4,3,2,1,0:T(8,128)(2,1)}, u32[]{:S(2)}) %copy-start.1) | copy-done | bytes 196632
  2.5 0.0 copy-start.2
  2.5 0.7 %copy-done.2 = f32[1,1,1024]{2,1,0:T(1,128)S(1)} copy-done((f32[1,1,1024]{2,1,0:T(1,128)S(1)}, f32[1,1,1024]{2,1,0:T(1,128)}, u32[]{:S(2)}) %copy-start.2) | copy-done | bytes 4120
  3.2 0.0 copy-start.3
  3.2 0.7 %copy-done.3 = s32[1,1024]{1,0:T(1,128)S(1)} copy-done((s32[1,1024]{1,0:T(1,128)S(1)}, s32[1,1024]{1,0:T(1,128)}, u32[]{:S(2)}) %copy-start.3) | copy-done | bytes 4120
  3.9 0.0 copy-start.4
  3.9 0.7 %copy-done.4 = f32[128]{0:T(128)S(1)} copy-done((f32[128]{0:T(128)S(1)}, f32[128]{0:T(128)}, u32[]{:S(2)}) %copy-start.4) | copy-done | bytes 536
  4.5 36.7 %shard_map.55 = bf16[1,1,2,48,1024]{4,3,2,1,0:T(8,128)(2,1)S(1)} custom-call(bf16[1,1,2,512,1024]{4,3,2,1,0:T(8,128)(2,1)S(1)} %copy-done, f32[1,1,1024]{2,1,0:T(1,128)S(1)} %copy-done.2, s32[1,1024]{1,0:T(1,128)S(1)} %copy-done.3, f32[128]{0:T(128)S(1)} %copy-done.4, bf16[1,1,2,48,1024]{4,3,2,1,0:T(8,128)(2,1)S(1)} %copy-done.1), custom_call_target="tpu_custom_call" | custom-call | tf_op jit(solution)/shard_map/pallas_call | solution.py:219
  41.3 0.7 %copy.7 = bf16[1,1,2,48,1024]{4,3,2,1,0:T(8,128)(2,1)} copy(bf16[1,1,2,48,1024]{4,3,2,1,0:T(8,128)(2,1)S(1)} %shard_map.55) | data formatting | bytes 393216
Async XLA Ops:
  0.0 1.6 %copy-start = (bf16[1,1,2,512,1024]{4,3,2,1,0:T(8,128)(2,1)S(1)}, bf16[1,1,2,512,1024]{4,3,2,1,0:T(8,128)(2,1)}, u32[]{:S(2)}) copy-start(bf16[1,1,2,512,1024]{4,3,2,1,0:T(8,128)(2,1)} %codes_hbm.1) | copy-start | bytes 6291460
  1.6 0.9 %copy-start.1 = (bf16[1,1,2,48,1024]{4,3,2,1,0:T(8,128)(2,1)S(1)}, bf16[1,1,2,48,1024]{4,3,2,1,0:T(8,128)(2,1)}, u32[]{:S(2)}) copy-start(bf16[1,1,2,48,1024]{4,3,2,1,0:T(8,128)(2,1)} %fields_hbm.1) | copy-start | bytes 589828
  2.5 0.7 %copy-start.2 = (f32[1,1,1024]{2,1,0:T(1,128)S(1)}, f32[1,1,1024]{2,1,0:T(1,128)}, u32[]{:S(2)}) copy-start(f32[1,1,1024]{2,1,0:T(1,128)} %scale_hbm.1) | copy-start | bytes 12292
  3.2 0.7 %copy-start.3 = (s32[1,1024]{1,0:T(1,128)S(1)}, s32[1,1024]{1,0:T(1,128)}, u32[]{:S(2)}) copy-start(s32[1,1024]{1,0:T(1,128)} %index_hbm.1) | copy-start | bytes 12292
  3.9 0.7 %copy-start.4 = (f32[128]{0:T(128)S(1)}, f32[128]{0:T(128)}, u32[]{:S(2)}) copy-start(f32[128]{0:T(128)} %table_hbm.1) | copy-start | bytes 1540

commit v2 on v1

--- a/solution.py
+++ b/solution.py
@@ -244,7 +244,7 @@
             dma((chunks,)),
             dma((chunks,)),
         ],
-        compiler_params=pltpu.CompilerParams(collective_id=0, has_side_effects=True, vmem_limit_bytes=40 * 2**20),
+        compiler_params=pltpu.CompilerParams(collective_id=0, has_side_effects=True, vmem_limit_bytes=67043328),
     )(codes, row_scale, refl_index, refl_table, fields_in)
 
 

time: 42.2 us -> 38.8 us (0.919)
  local copies, waits for them, and re-layouts: 5.22 us -> 1.62 us
    unnamed x11 -> x1, local copies, waits for them, and re-layouts: 5.22 us -> 1.62 us
where the time goes in v2:
time: 38.8 us; the launch traced here: 38.6 us
  Pallas kernels  37 us (95%)
  local copies, waits for them, and re-layouts  1.62 us (4%)
    pallas_call x1, Pallas kernels, shards(): pl.pallas_call(functools.partial(kernel, levels, halves, chunks, rows), o...  37 us
    unnamed x1, local copies, waits for them, and re-layouts  1.62 us

profile of v2, /device:TPU:6, one launch (start us, length us, event | category | flops | bytes accessed | tf_op | source)
XLA Modules:
  0.0 38.6 jit_solution(17674025435932767529)
XLA Ops:
  0.0 37.0 %shard_map.55 = bf16[1,1,2,48,1024]{4,3,2,1,0:T(8,128)(2,1)} custom-call(bf16[1,1,2,512,1024]{4,3,2,1,0:T(8,128)(2,1)} %codes_hbm.1, f32[1,1,1024]{2,1,0:T(1,128)} %scale_hbm.1, s32[1,1024]{1,0:T(1,128)} %index_hbm.1, f32[128]{0:T(128)} %table_hbm.1, bf16[1,1,2,48,1024]{4,3,2,1,0:T(8,128)(2,1)} %fields_hbm.1), custom_call_target="tpu_custom_call" | custom-call | tf_op jit(solution)/shard_map/pallas_call | solution.py:219
  37.0 1.6 %copy.7 = bf16[1,1,2,48,1024]{4,3,2,1,0:T(8,128)(2,1)} copy(bf16[1,1,2,48,1024]{4,3,2,1,0:T(8,128)(2,1)} %shard_map.55) | data formatting | bytes 393216

commit v3 on v2

--- a/solution.py
+++ b/solution.py
@@ -13,7 +13,7 @@
 
 def kernel(levels, halves, chunks, rows, codes_hbm, scale_hbm, index_hbm, table_hbm, fields_hbm, out_ref,
            own, weights, fields, source, reflect, scale, index, table, chain, side, partner, result,
-           load_sem, code_sem, code_send, code_recv, chain_send, chain_recv, side_send, side_recv, part_send):
+           load_sem, code_sem, code_send, code_recv, chain_send, chain_recv, side_send, side_recv, part_send, ready):
     depth = lax.axis_index("depth")
     slot = lax.axis_index("dirfreq")
     core = lax.axis_index("shot")
@@ -27,9 +27,8 @@
     has_prev = jnp.where(is_down, jnp.logical_not(first), jnp.logical_not(last))
     has_side = jnp.logical_or(is_down, jnp.logical_not(first))
     down_next = jnp.logical_and(is_down, jnp.logical_not(last))
-    up_prev = jnp.logical_and(is_up, jnp.logical_not(first))
     blocks = own.shape[1] // BLOCK
-    half = 2 * rows
+    part_width = own.shape[1]
 
     small = [pltpu.make_async_copy(a, b, load_sem.at[i]) for i, (a, b) in enumerate(
         ((index_hbm, index), (table_hbm, table), (scale_hbm, scale), (fields_hbm, fields)))]
@@ -59,14 +58,6 @@
     @pl.when(has_prev)
     def _():
         greet({"depth": behind})
-
-    @pl.when(down_next)
-    def _():
-        greet({"depth": depth + 1, "dirfreq": across})
-
-    @pl.when(up_prev)
-    def _():
-        greet({"depth": depth - 1, "dirfreq": across})
 
     for copy in small[:2]:
         copy.wait()
@@ -88,20 +79,29 @@
             for t in range(per):
                 source[m * per + t, p * rows:(p + 1) * rows] = values[t * rows:(t + 1) * rows]
 
-    wanted = (2 + has_next.astype(jnp.int32) + has_prev.astype(jnp.int32)
-              + jnp.logical_or(down_next, up_prev).astype(jnp.int32))
-    pl.semaphore_wait(barrier, wanted)
-
-    def part_copy(k):
-        return pltpu.make_async_remote_copy(
-            src_ref=partner.at[k], dst_ref=side.at[k], send_sem=part_send.at[k], recv_sem=side_recv.at[k],
+    pl.semaphore_wait(barrier, 2 + has_next.astype(jnp.int32) + has_prev.astype(jnp.int32))
+
+    @pl.when(jnp.logical_and(is_down, has_prev))
+    def _():
+        pl.semaphore_signal(ready, inc=1, device_id={"depth": behind}, device_id_type=MESH)
+
+    def span_of(h):
+        return pl.ds(pl.multiple_of(h * part_width, BLOCK), part_width)
+
+    def part_copy(k, h):
+        return pltpu.make_async_remote_copy(
+            src_ref=partner.at[k, h], dst_ref=side.at[k, h], send_sem=part_send.at[k, h], recv_sem=side_recv.at[k, h],
             device_id={"dirfreq": across}, device_id_type=MESH)
 
+    both = [(0, core), (1, 1 - core)]
+
     @pl.when(is_up)
     def _():
         for k in range(chunks):
-            partner[k] = (-reflect[...] * source[k]).astype(jnp.bfloat16)
-            part_copy(k).start()
+            for _, h in both:
+                span = span_of(h)
+                partner[k, h] = (-reflect[:, span] * source[k, :, span]).astype(jnp.bfloat16)
+                part_copy(k, h).start()
 
     @pl.when(jnp.logical_not(has_prev))
     def _():
@@ -128,52 +128,70 @@
         weights[core, q, p] = own[p, q * BLOCK:(q + 1) * BLOCK].T
         code_copy(q, p).start()
 
-    def chain_copy(k):
-        return pltpu.make_async_remote_copy(
-            src_ref=result.at[k], dst_ref=chain.at[k], send_sem=chain_send.at[k], recv_sem=chain_recv.at[k],
+    def chain_copy(k, h):
+        return pltpu.make_async_remote_copy(
+            src_ref=result.at[k, h], dst_ref=chain.at[k, h], send_sem=chain_send.at[k, h], recv_sem=chain_recv.at[k, h],
             device_id={"depth": ahead}, device_id_type=MESH)
 
-    def side_copy(k):
-        return pltpu.make_async_remote_copy(
-            src_ref=result.at[k], dst_ref=side.at[k], send_sem=side_send.at[k], recv_sem=side_recv.at[k],
+    def side_copy(k, h):
+        return pltpu.make_async_remote_copy(
+            src_ref=result.at[k, h], dst_ref=side.at[k, h], send_sem=side_send.at[k, h], recv_sem=side_recv.at[k, h],
             device_id={"depth": depth + 1, "dirfreq": across}, device_id_type=MESH)
 
     sign = jnp.where(is_down, 1.0, -1.0).astype(jnp.float32)
 
-    def step(k, opening):
+    def mixed_half(k, h):
         @pl.when(has_side)
         def _():
-            part_copy(k).wait_recv()
+            part_copy(k, h).wait_recv()
 
         @pl.when(has_prev)
         def _():
-            chain_copy(k).wait_recv()
-
-        beside = side[k].astype(jnp.float32)
-        base = jnp.where(is_down, beside + source[k],
-                         (reflect[...] * beside).astype(jnp.bfloat16).astype(jnp.float32))
-        mixed = ((1.0 + sign * reflect[...]) * chain[k].astype(jnp.float32) + base).astype(jnp.bfloat16)
-        for t in range(2):
-            holder = core if t == 0 else 1 - core
+            chain_copy(k, h).wait_recv()
+
+        span = span_of(h)
+        ratio = reflect[:, span]
+        beside = side[k, h].astype(jnp.float32)
+        base = jnp.where(is_down, beside + source[k, :, span],
+                         (ratio * beside).astype(jnp.bfloat16).astype(jnp.float32))
+        return ((1.0 + sign * ratio) * chain[k, h].astype(jnp.float32) + base).astype(jnp.bfloat16)
+
+    def step(k, opening):
+        sums = {}
+        early, late = both[0][1], both[1][1]
+        mixed = mixed_half(k, early)
+        for t, holder in both:
             for q in range(blocks):
                 if opening and t == 1:
                     code_arrival(q, 0).wait_recv()
                     code_arrival(q, 1).wait_recv()
-                by_real = jnp.dot(mixed, weights[holder, q, 0], preferred_element_type=jnp.float32)
-                by_imag = jnp.dot(mixed, weights[holder, q, 1], preferred_element_type=jnp.float32)
+                for p in range(2):
+                    sums[t, q, p] = jnp.dot(mixed, weights[holder, q, p, span_of(early)],
+                                            preferred_element_type=jnp.float32)
+        mixed = mixed_half(k, late)
+        if opening:
+            @pl.when(down_next)
+            def _():
+                pl.semaphore_wait(ready, 1)
+
+        for t, holder in both:
+            for q in range(blocks):
+                by_real, by_imag = (
+                    sums[t, q, p] + jnp.dot(mixed, weights[holder, q, p, span_of(late)],
+                                            preferred_element_type=jnp.float32) for p in range(2))
                 real = by_real[:rows] - by_imag[rows:]
                 imag = by_imag[:rows] + by_real[rows:]
                 columns = pl.ds(pl.multiple_of((holder * blocks + q) * BLOCK, BLOCK), BLOCK)
-                both = jnp.concatenate([real, imag], axis=0) * scale[0, :, columns]
-                result[k, :, columns] = both.astype(jnp.bfloat16)
-
-        @pl.when(has_next)
-        def _():
-            chain_copy(k).start()
-
-        @pl.when(down_next)
-        def _():
-            side_copy(k).start()
+                pair = jnp.concatenate([real, imag], axis=0) * scale[0, :, columns]
+                result[k, holder, :, q * BLOCK:(q + 1) * BLOCK] = pair.astype(jnp.bfloat16)
+
+            @pl.when(has_next)
+            def _():
+                chain_copy(k, holder).start()
+
+            @pl.when(down_next)
+            def _():
+                side_copy(k, holder).start()
 
     step(0, True)
 
@@ -182,27 +200,25 @@
         step(k, False)
 
     for m in range(chunks // per):
-        for p in range(2):
-            parts = [result[m * per + t].astype(jnp.float32)[p * rows:(p + 1) * rows] for t in range(per)]
-            out_ref[0, 0, p, m * 16:(m + 1) * 16] = jnp.concatenate(parts, axis=0).astype(jnp.bfloat16)
+        for h in range(2):
+            for p in range(2):
+                parts = [result[m * per + t, h].astype(jnp.float32)[p * rows:(p + 1) * rows] for t in range(per)]
+                out_ref[0, 0, p, m * 16:(m + 1) * 16, h * part_width:(h + 1) * part_width] = (
+                    jnp.concatenate(parts, axis=0).astype(jnp.bfloat16))
 
     for q, p in pieces:
         code_copy(q, p).wait_send()
 
-    @pl.when(is_up)
-    def _():
-        for k in range(chunks):
-            part_copy(k).wait_send()
-
-    @pl.when(has_next)
-    def _():
-        for k in range(chunks):
-            chain_copy(k).wait_send()
-
-    @pl.when(down_next)
-    def _():
-        for k in range(chunks):
-            side_copy(k).wait_send()
+    def drain(flag, copy):
+        @pl.when(flag)
+        def _():
+            for k in range(chunks):
+                for h in range(2):
+                    copy(k, h).wait_send()
+
+    drain(is_up, part_copy)
+    drain(has_next, chain_copy)
+    drain(down_next, side_copy)
 
 
 def shards(codes, row_scale, refl_index, refl_table, fields_in):
@@ -215,6 +231,7 @@
     blocks = held // BLOCK
     dma = pltpu.SemaphoreType.DMA
     wave = (chunks, 2 * rows, width)
+    halved = (chunks, 2, 2 * rows, held)
     any_space = pl.BlockSpec(memory_space=pltpu.HBM)
     return pl.pallas_call(
         functools.partial(kernel, levels, halves, chunks, rows),
@@ -230,19 +247,20 @@
             pltpu.VMEM(row_scale.shape, jnp.float32),
             pltpu.VMEM(refl_index.shape, jnp.int32),
             pltpu.VMEM(refl_table.shape, jnp.float32),
-            pltpu.VMEM(wave, jnp.bfloat16),
-            pltpu.VMEM(wave, jnp.bfloat16),
-            pltpu.VMEM(wave, jnp.bfloat16),
-            pltpu.VMEM(wave, jnp.bfloat16),
+            pltpu.VMEM(halved, jnp.bfloat16),
+            pltpu.VMEM(halved, jnp.bfloat16),
+            pltpu.VMEM(halved, jnp.bfloat16),
+            pltpu.VMEM(halved, jnp.bfloat16),
             dma((4,)),
             dma((blocks, 2)),
             dma((blocks, 2)),
             dma((blocks, 2)),
-            dma((chunks,)),
-            dma((chunks,)),
-            dma((chunks,)),
-            dma((chunks,)),
-            dma((chunks,)),
+            dma((chunks, 2)),
+            dma((chunks, 2)),
+            dma((chunks, 2)),
+            dma((chunks, 2)),
+            dma((chunks, 2)),
+            pltpu.SemaphoreType.REGULAR,
         ],
         compiler_params=pltpu.CompilerParams(collective_id=0, has_side_effects=True, vmem_limit_bytes=67043328),
     )(codes, row_scale, refl_index, refl_table, fields_in)

time: 38.8 us -> 38.2 us (0.985)
  Pallas kernels: 37 us -> 36.4 us
    pallas_call x1, Pallas kernels: 37 us -> 36.4 us  [shards(): pl.pallas_call(functools.partial(kernel, levels, halves, chunks, rows), o...]
where the time goes in v3:
time: 38.2 us; the launch traced here: 38 us
  Pallas kernels  36.4 us (95%)
  local copies, waits for them, and re-layouts  1.62 us (4%)
    pallas_call x1, Pallas kernels, shards(): pl.pallas_call(functools.partial(kernel, levels, halves, chunks, rows), o...  36.4 us
    unnamed x1, local copies, waits for them, and re-layouts  1.62 us

profile of v3, /device:TPU:6, one launch (start us, length us, event | category | flops | bytes accessed | tf_op | source)
XLA Modules:
  0.0 38.0 jit_solution(3652790889519597949)
XLA Ops:
  0.0 36.4 %shard_map.55 = bf16[1,1,2,48,1024]{4,3,2,1,0:T(8,128)(2,1)} custom-call(bf16[1,1,2,512,1024]{4,3,2,1,0:T(8,128)(2,1)} %codes_hbm.1, f32[1,1,1024]{2,1,0:T(1,128)} %scale_hbm.1, s32[1,1024]{1,0:T(1,128)} %index_hbm.1, f32[128]{0:T(128)} %table_hbm.1, bf16[1,1,2,48,1024]{4,3,2,1,0:T(8,128)(2,1)} %fields_hbm.1), custom_call_target="tpu_custom_call" | custom-call | tf_op jit(solution)/shard_map/pallas_call | solution.py:236
  36.4 1.6 %copy.7 = bf16[1,1,2,48,1024]{4,3,2,1,0:T(8,128)(2,1)} copy(bf16[1,1,2,48,1024]{4,3,2,1,0:T(8,128)(2,1)} %shard_map.55) | data formatting | bytes 393216
